TPU v7x, 32 devices: a whole 2x2x4 slice. The times are simulated.
32 devices in a mesh: ka: 8 (over z, core), band: 4 (over y, x).
Axes of the slice: x: 2, y: 2, z: 4, core: 2. Of those that a mesh axis runs over, the one named last changes fastest.
Arguments:
- occ_rows: bfloat16 [8, 2048, 128], P('ka', 'band'), may hold values from -0.5 to 0.5
- vir_rows: bfloat16 [8, 2048, 896], P('ka', 'band'), may hold values from -0.1875 to 0.1875
- trial_vectors: float32 [8, 2, 128, 896], P('ka', None, None, 'band'), may hold values from -6 to 6
- occ_energy: float32 [8, 128], P('ka'), may hold values from -1.2 to -0.3
- vir_energy: float32 [8, 896], P('ka', 'band'), may hold values from 0.1 to 1.5
- coulomb: bfloat16 [2048, 2048], P('band'), may hold values from -0.09375 to 0.09375
- exch_kernel: bfloat16 [8, 2048, 2048], P(None, 'band'), as said below
- minus_table: int32 [8, 8], replicated, may hold values from 0 to 7, as said below
Outputs:
- sigma_vectors: float32 [8, 2, 128, 896], P('ka', None, None, 'band')
Inputs may be any that keep to these rules, and one draw needn't show every extreme that they name: minus_table[k, q] is the k-point k - q on a group of 8 k-points: every row and every column holds each index once, and one q gives minus_table[k, q] == k for every k. Each exch_kernel[q] is symmetric.
All inputs are finite; a program needn't handle non-finite values.
Results may differ from a plain program's by a relative error of at most 0.0051.
Values may be sent and summed in bfloat16 or wider, within the bound.
No kernel may reach another device: no remote copies, remote signals or barrier semaphores. Data moves between devices by JAX's collectives and lax.ppermute only.
A program may use at most 128 MiB of HBM per device.

v0:
```python
import jax
import jax.numpy as jnp
from jax import lax
from jax.sharding import PartitionSpec as P


def per_device(
    occ_rows, vir_rows, trial_vectors, occ_energy, vir_energy, coulomb, exch_kernel, minus_table
):
    vectors = trial_vectors.shape[1]
    own_rows = occ_rows.shape[1]
    kpoints = lax.axis_size("ka")
    self_point = lax.axis_index("ka")
    trial_half = trial_vectors[0].astype(jnp.bfloat16)
    trial_full, vir_full = (
        lax.all_gather(trial_half, "band", axis=2, tiled=True),
        lax.all_gather(vir_rows[0], "band", axis=0, tiled=True),
    )
    auxiliary = vir_full.shape[0]
    occ_own = occ_rows[0]
    vir_own = vir_rows[0]
    mixed_rows = jnp.einsum(
        "ri,via->vra", occ_own, trial_full, preferred_element_type=jnp.float32
    ).astype(jnp.bfloat16)
    pair_block = jnp.einsum(
        "vra,na->vrn", mixed_rows, vir_full, preferred_element_type=jnp.float32
    ).astype(jnp.bfloat16)
    density_own = jnp.sum(
        mixed_rows.astype(jnp.float32) * vir_own.astype(jnp.float32)[None], axis=2
    )
    density_sum = lax.psum(density_own, "ka")
    density_half = lax.all_gather(density_sum.astype(jnp.bfloat16), "band", axis=1, tiled=True)
    potential = jnp.einsum("vn,rn->vr", density_half, coulomb, preferred_element_type=jnp.float32)
    piece_width = auxiliary // kpoints
    kernel_cols = lax.dynamic_slice_in_dim(exch_kernel, self_point * piece_width, piece_width, 2)
    split_pairs = pair_block.reshape(vectors, own_rows, kpoints, piece_width)
    moved_pairs = jnp.take(
        lax.all_to_all(split_pairs, "ka", split_axis=2, concat_axis=2, tiled=True),
        minus_table,
        axis=2,
    )
    summed = jnp.einsum(
        "vrkqc,qrc->vrkc", moved_pairs, kernel_cols, preferred_element_type=jnp.float32
    )
    screened = lax.all_to_all(
        summed.astype(jnp.bfloat16), "ka", split_axis=2, concat_axis=2, tiled=True
    )
    screened = screened.reshape(vectors, own_rows, auxiliary)
    product = jnp.einsum("vrn,na->vra", screened, vir_full, preferred_element_type=jnp.float32)
    weights = (2.0 * potential[:, :, None] * vir_own.astype(jnp.float32)[None] - product).astype(
        jnp.bfloat16
    )
    partial_sums = jnp.einsum("ri,vra->via", occ_own, weights, preferred_element_type=jnp.float32)
    coupled = lax.psum_scatter(partial_sums, "band", scatter_dimension=2, tiled=True)
    energy_gaps = vir_energy[0][None, :] - occ_energy[0][:, None]
    return (energy_gaps[None] * trial_vectors[0] + coupled)[None]


def solution(mesh):
    in_specs = (
        P("ka", "band", None),
        P("ka", "band", None),
        P("ka", None, None, "band"),
        P("ka", None),
        P("ka", "band"),
        P("band", None),
        P(None, "band", None),
        P(),
    )
    out_specs = P("ka", None, None, "band")
    return jax.shard_map(
        per_device, mesh=mesh, in_specs=in_specs, out_specs=out_specs, check_vma=False
    )
```

profile of v0, /device:TPU:0, one launch (start us, length us, event | category | flops | bytes accessed | tf_op | source)
XLA Modules:
  0.0 375.4 jit_solution(881767993368550166)
XLA Ops:
  6.5 0.7 all-gather.3.cloned.1.call-update
  7.3 2.6 bitcast_convert_fusion.1
  9.9 2.8 copy.14
  12.7 13.6 %all_gather.9 = bf16[2,128,896]{1,2,0:T(8,128)(2,1)S(1)} all-gather(bf16[2,128,224]{1,2,0:T(8,128)(2,1)S(1)} %bitcast_convert_fusion.2), channel_id=1, replica_groups=mesh['ka'=8,'band'=4] {'band'}, dimensions={2}, use_global_device_ids=true | all-gather | bytes 573440 | tf_op jit(solution)/shard_map/all_gather | solution.py:16
  26.3 3.4 multiply_reduce_fusion.1
  29.7 31.7 %all-gather.3.cloned.1.call-done = bf16[1,2048,896]{2,1,0:T(8,128)(2,1)} async-done(((bf16[1,512,896]{2,1,0:T(8,128)(2,1)}), bf16[1,2048,896]{2,1,0:T(8,128)(2,1)}) %all-gather.3.cloned.1.call-update) | async-done | bytes 3670032 | tf_op jit(solution)/shard_map/all_gather | solution.py:17
  61.4 7.1 %convolution_convert_fusion = bf16[2,512,2048]{2,1,0:T(8,128)(2,1)S(1)} fusion(bf16[1,2048,896]{2,1,0:T(8,128)(2,1)} %all-gather.3.cloned.1.call-done, bf16[2,896,512]{2,1,0:T(8,128)(2,1)} %get-tuple-element.6), kind=kOutput, calls=%fused_computation.4 | convolution fusion | flops 3760193536 | bytes 9699328 | tf_op jit(solution)/shard_map/vra,na->vrn/dot_general | solution.py:25
  68.5 2.4 copy.35
  70.9 4.7 %all-to-all-start = ((bf16[2,512,8,256]{3,1,0,2:T(8,128)(2,1)}), bf16[2,512,8,256]{3,1,0,2:T(8,128)(2,1)}, u32[]{:S(2)}, u32[]{:S(2)}) async-start(bf16[2,512,8,256]{3,1,0,2:T(8,128)(2,1)} %bitcast.58), calls=%async_computation | async-start | bytes 8388608 | tf_op jit(solution)/shard_map/all_to_all | solution.py:38
  75.8 4.0 %bitcast_convert_fusion = f32[512,256,8]{1,0,2:T(8,128)} fusion(bf16[8,512,2048]{2,1,0:T(8,128)(2,1)} %param.14, s32[]{:T(128)S(6)} %select_n.12), kind=kLoop, calls=%fused_computation.10 | loop fusion | flops 1048576 | bytes 6291460
  79.8 89.9 %all-to-all-done = bf16[2,512,8,256]{3,1,0,2:T(8,128)(2,1)} async-done(((bf16[2,512,8,256]{3,1,0,2:T(8,128)(2,1)}), bf16[2,512,8,256]{3,1,0,2:T(8,128)(2,1)}, u32[]{:S(2)}, u32[]{:S(2)}) %all-to-all-start) | async-done | bytes 4194336 | tf_op jit(solution)/shard_map/all_to_all | solution.py:38
  169.7 4.5 %copy.17 = bf16[2,512,8,256]{3,1,2,0:T(8,128)(2,1)} copy(bf16[2,512,8,256]{3,1,0,2:T(8,128)(2,1)} %all-to-all-done) | data formatting | bytes 8388608 | tf_op jit(solution)/shard_map/all_to_all | solution.py:38
  174.2 14.6 %gather_fusion = bf16[64,2,512,256]{3,2,1,0:T(8,128)(2,1)} fusion(bf16[2,512,8,256]{3,1,2,0:T(8,128)(2,1)} %copy.17, s32[1024]{0:T(1024)S(1)} %pad_clamp_fusion), kind=kCustom, calls=%fused_computation | custom fusion | bytes 67109120 | tf_op jit(solution)/shard_map/jit(_take)/gather | solution.py:37
  188.8 19.3 %multiply_reduce_fusion = bf16[512,256,2,8]{1,0,2,3:T(8,128)(2,1)} fusion(f32[512,256,8]{1,0,2:T(8,128)} %bitcast_convert_fusion, bf16[8,8,2,512,256]{4,3,2,1,0:T(8,128)(2,1)} %bitcast.57, pred[8,8]{1,0:T(8,128)(4,1)S(1)} %compare_and_fusion), kind=kLoop, calls=%fused_computation.1 | loop fusion | flops 65011712 | bytes 41943104
  208.1 6.5 %copy.29 = bf16[512,256,2,8]{0,1,2,3:T(8,128)(2,1)} copy(bf16[512,256,2,8]{1,0,2,3:T(8,128)(2,1)} %multiply_reduce_fusion) | data formatting | bytes 8388608 | tf_op jit(solution)/shard_map/vrkqc,qrc->vrkc/dot_general | solution.py:42
  214.6 4.6 %all-to-all-start.1 = ((bf16[2,512,8,256]{1,3,0,2:T(8,128)(2,1)}), bf16[2,512,8,256]{1,3,0,2:T(8,128)(2,1)}, u32[]{:S(2)}, u32[]{:S(2)}) async-start(bf16[2,512,8,256]{1,3,0,2:T(8,128)(2,1)} %bitcast.59), calls=%async_computation.1 | async-start | bytes 8388608 | tf_op jit(solution)/shard_map/all_to_all | solution.py:45
  219.2 80.0 %psum.7 = bf16[2,512]{1,0:T(2,128)(2,1)S(1)} all-reduce(f32[2,512]{1,0:T(2,128)S(1)} %get-tuple-element.5), channel_id=1, replica_groups=mesh['ka'=8,'band'=4] {'ka'}, use_global_device_ids=true, to_apply=%region_1.0 | all-reduce | flops 1024 | bytes 6144 | tf_op jit(solution)/shard_map/psum | solution.py:31
  299.2 8.2 %all_gather.10 = bf16[2,2048]{1,0:T(2,128)(2,1)S(1)} all-gather(bf16[2,512]{1,0:T(2,128)(2,1)S(1)} %psum.7), channel_id=1, replica_groups=mesh['ka'=8,'band'=4] {'band'}, dimensions={1}, use_global_device_ids=true | all-gather | bytes 10240 | tf_op jit(solution)/shard_map/all_gather | solution.py:32
  307.4 0.6 convolution_multiply_fusion
  308.1 5.2 %all-to-all-done.1 = bf16[2,512,8,256]{1,3,0,2:T(8,128)(2,1)} async-done(((bf16[2,512,8,256]{1,3,0,2:T(8,128)(2,1)}), bf16[2,512,8,256]{1,3,0,2:T(8,128)(2,1)}, u32[]{:S(2)}, u32[]{:S(2)}) %all-to-all-start.1) | async-done | bytes 4194336 | tf_op jit(solution)/shard_map/all_to_all | solution.py:45
  313.3 4.5 %copy.18 = bf16[2,512,8,256]{1,3,2,0:T(8,128)(2,1)} copy(bf16[2,512,8,256]{1,3,0,2:T(8,128)(2,1)} %all-to-all-done.1) | data formatting | bytes 8388608 | tf_op jit(solution)/shard_map/all_to_all | solution.py:45
  317.8 9.3 %fusion.7 = f32[2,128,896]{1,2,0:T(8,128)} fusion(f32[2,512]{1,0:T(2,128)S(1)} %convolution_multiply_fusion, f32[512,896]{0,1:T(8,128)} %copy.14, bf16[2,512,2048]{1,2,0:T(8,128)(2,1)} %bitcast.60, bf16[1,2048,896]{2,1,0:T(8,128)(2,1)} %all-gather.3.cloned.1.call-done, bf16[1,512,128]{2,1,0:T(8,128)(2,1)S(1)} %copy-done.2), kind=kOutput, calls=%fused_computation.16 | convolution fusion | flops 3995729920 | bytes 10752000 | tf_op jit(solution)/shard_map/ri,vra->via/dot_general | solution.py:53
  327.2 39.7 %reduce-scatter.2.cloned.1.call-done = f32[2,128,224]{1,2,0:T(8,128)} async-done(((f32[2,128,896]{1,2,0:T(8,128)}), f32[2,128,224]{1,2,0:T(8,128)}) %reduce-scatter.2.cloned.1.call-update) | async-done | bytes 229392 | tf_op jit(solution)/shard_map/reduce_scatter | solution.py:54
  366.9 1.7 fusion.13
  (21 shorter events, 0.3 us)
Async XLA Ops:
  6.5 300.9 %copy-start = (bf16[512,2048]{1,0:T(8,128)(2,1)S(1)}, bf16[512,2048]{1,0:T(8,128)(2,1)}, u32[]{:S(2)}) copy-start(bf16[512,2048]{1,0:T(8,128)(2,1)} %param.13) | copy-start | bytes 6291460
  6.5 6.1 %copy-start.1 = (f32[1,2,128,224]{2,3,1,0:T(8,128)S(1)}, f32[1,2,128,224]{2,3,1,0:T(8,128)}, u32[]{:S(2)}) copy-start(f32[1,2,128,224]{2,3,1,0:T(8,128)} %param.10) | copy-start | bytes 688132
  6.5 54.8 %all-gather.3.cloned.1.call-start = ((), (), s32[]{:S(2)}) async-start(), calls=%async_computation.4 | async-start | bytes 4587520 | tf_op jit(solution)/shard_map/all_gather | solution.py:17
  7.3 19.0 %copy-start.2 = (bf16[1,512,128]{2,1,0:T(8,128)(2,1)S(1)}, bf16[1,512,128]{2,1,0:T(8,128)(2,1)}, u32[]{:S(2)}) copy-start(bf16[1,512,128]{2,1,0:T(8,128)(2,1)} %param.8) | copy-start | bytes 393220
  70.9 4.7 %copy-start.3 = (s32[8,8]{1,0:T(8,128)S(1)}, s32[8,8]{1,0:T(8,128)}, u32[]{:S(2)}) copy-start(s32[8,8]{1,0:T(8,128)} %param.15) | copy-start | bytes 772
  70.9 98.8 %all-to-all-start = ((bf16[2,512,8,256]{3,1,0,2:T(8,128)(2,1)}), bf16[2,512,8,256]{3,1,0,2:T(8,128)(2,1)}, u32[]{:S(2)}, u32[]{:S(2)}) async-start(bf16[2,512,8,256]{3,1,0,2:T(8,128)(2,1)} %bitcast.58), calls=%async_computation | async-start | bytes 8388608 | tf_op jit(solution)/shard_map/all_to_all | solution.py:38
  214.6 98.7 %all-to-all-start.1 = ((bf16[2,512,8,256]{1,3,0,2:T(8,128)(2,1)}), bf16[2,512,8,256]{1,3,0,2:T(8,128)(2,1)}, u32[]{:S(2)}, u32[]{:S(2)}) async-start(bf16[2,512,8,256]{1,3,0,2:T(8,128)(2,1)} %bitcast.59), calls=%async_computation.1 | async-start | bytes 8388608 | tf_op jit(solution)/shard_map/all_to_all | solution.py:45
  219.1 147.8 %reduce-scatter.2.cloned.1.call-start = ((), (), s32[]{:S(2)}) async-start(), calls=%async_computation.3 | async-start | bytes 1146880 | tf_op jit(solution)/shard_map/reduce_scatter | solution.py:54
  317.8 9.3 %copy-start.4 = (f32[1,224]{1,0:T(1,128)S(1)}, f32[1,224]{1,0:T(1,128)}, u32[]{:S(2)}) copy-start(f32[1,224]{1,0:T(1,128)} %param.12) | copy-start | bytes 2692
  317.8 9.3 %copy-start.5 = (f32[1,128]{1,0:T(1,128)S(1)}, f32[1,128]{1,0:T(1,128)}, u32[]{:S(2)}) copy-start(f32[1,128]{1,0:T(1,128)} %param.11) | copy-start | bytes 1540
Sparse Core Ops, SparseCore 0:
  9.2 52.1 all-gather.2
  327.2 39.6 reduce-scatter.1
where the time goes:
time: 376 us; the launch traced here: 375 us
  waiting for transfers between devices  167 us (44%)
  blocking collectives  102 us (27%)
  local copies, waits for them, and re-layouts  35.4 us (9%)
  other arithmetic  27.7 us (7%)
  matrix products  20.5 us (5%)
  between operations  13.5 us (4%)
  starting transfers between devices  9.34 us (2%)
    all_to_all x1, waiting for transfers between devices, per_device(): lax.all_to_all(split_pairs, 'ka', split_axis=2, concat_axis=2, tiled=True)  89.9 us
    psum x1, blocking collectives, per_device(): density_sum = lax.psum(density_own, 'ka')  80 us
    reduce_scatter x1, waiting for transfers between devices, per_device(): lax.psum_scatter(partial_sums, 'band', scatter_dimension=2, tiled=True)  39.7 us
    all_gather x1, waiting for transfers between devices, per_device(): lax.all_gather(vir_rows[0], 'band', axis=0, tiled=True)  31.7 us
    unnamed x2, other arithmetic  23.3 us
    gather x1, local copies, waits for them, and re-layouts, per_device(): jnp.take(lax.all_to_all(split_pairs, 'ka', split_axis=2, concat_axis=2, t...  14.6 us
    all_gather x1, blocking collectives, per_device(): lax.all_gather(trial_half, 'band', axis=2, tiled=True)  13.6 us
    dot_general x1, matrix products, per_device(): jnp.einsum('ri,vra->via', occ_own, weights, preferred_element_type=jnp.fl...  9.3 us
  transfers between devices with their start and end apart: 4, of which 4 were waited for; matrix products, arithmetic and copies ran while one was open for 4% of the time, Pallas kernels for 0%

commit v1 on v0

v1 whole, which is shorter than its diff:
```python
import functools

import jax
import jax.numpy as jnp
from jax import lax
from jax.experimental import pallas as pl
from jax.experimental.pallas import tpu as pltpu
from jax.sharding import PartitionSpec as P


def exchange_kernel(
    self_ref, table_ref, y_ref, occ_ref, exch_ref, z_ref, where_ref, wide_ref, pair_ref, scr_ref, acc_ref
):
    kpoints, points, width = y_ref.shape
    tile, nocc = occ_ref.shape[1], occ_ref.shape[2]
    vectors = width // nocc
    step = pl.program_id(0)

    @pl.when(step == 0)
    def _():
        for k in range(kpoints):
            for q in range(kpoints):
                where_ref[k, table_ref[k, q]] = q
        acc_ref[...] = jnp.zeros_like(acc_ref)

    for k in range(kpoints):
        wide_ref[k] = exch_ref[k].astype(jnp.float32)
        stacked = jnp.concatenate(
            [y_ref[k, :, v * nocc : (v + 1) * nocc] for v in range(vectors)], axis=0
        )
        pair_ref[k] = lax.dot_general(
            stacked, occ_ref[k], (((1,), (1,)), ((), ())), preferred_element_type=jnp.float32
        )
    rows, lanes = 16, 128
    for r in range(points // rows):
        @pl.loop(0, tile // lanes)
        def _(c):
            cols = pl.ds(pl.multiple_of(c * lanes, lanes), lanes)
            held = [
                [pair_ref[m, pl.ds(v * points + r * rows, rows), cols] for m in range(kpoints)]
                for v in range(vectors)
            ]
            for k in range(kpoints):
                total = [None] * vectors
                for m in range(kpoints):
                    kern = wide_ref[where_ref[k, m], pl.ds(r * rows, rows), cols]
                    for v in range(vectors):
                        term = held[v][m] * kern
                        total[v] = term if total[v] is None else total[v] + term
                for v in range(vectors):
                    scr_ref[k, pl.ds(v * points + r * rows, rows), cols] = total[v].astype(jnp.bfloat16)
    for k in range(kpoints):
        acc_ref[k] += jnp.dot(scr_ref[k], occ_ref[k], preferred_element_type=jnp.float32)

    @pl.when(step == pl.num_programs(0) - 1)
    def _():
        for k in range(kpoints):
            for v in range(vectors):
                z_ref[k, :, v * nocc : (v + 1) * nocc] = acc_ref[
                    k, v * points : (v + 1) * points, :
                ].astype(z_ref.dtype)


def exchange(self_point, table, y_all, occ_all, exch):
    kpoints, points, width = y_all.shape
    auxiliary, nocc = occ_all.shape[1], occ_all.shape[2]
    tile = min(256, auxiliary)
    stacked = points * width // nocc
    grid_spec = pltpu.PrefetchScalarGridSpec(
        num_scalar_prefetch=2,
        grid=(auxiliary // tile,),
        in_specs=[
            pl.BlockSpec((kpoints, points, width), lambda t, s, tab: (0, 0, 0)),
            pl.BlockSpec((kpoints, tile, nocc), lambda t, s, tab: (0, t, 0)),
            pl.BlockSpec((kpoints, points, tile), lambda t, s, tab: (0, s[0], t)),
        ],
        out_specs=pl.BlockSpec((kpoints, points, width), lambda t, s, tab: (0, 0, 0)),
        scratch_shapes=[
            pltpu.SMEM((kpoints, kpoints), jnp.int32),
            pltpu.VMEM((kpoints, points, tile), jnp.float32),
            pltpu.VMEM((kpoints, stacked, tile), jnp.float32),
            pltpu.VMEM((kpoints, stacked, tile), jnp.bfloat16),
            pltpu.VMEM((kpoints, stacked, nocc), jnp.float32),
        ],
    )
    flops = 4 * kpoints * stacked * auxiliary * nocc
    return pl.pallas_call(
        exchange_kernel,
        grid_spec=grid_spec,
        out_shape=jax.ShapeDtypeStruct((kpoints, points, width), jnp.bfloat16),
        compiler_params=pltpu.CompilerParams(dimension_semantics=("arbitrary",)),
        cost_estimate=pl.CostEstimate(
            flops=16 * flops,
            bytes_accessed=2 * kpoints * auxiliary * (nocc + points),
            transcendentals=0,
        ),
    )(self_point, table, y_all, occ_all, exch)


def per_device(
    occ_rows, vir_rows, trial_vectors, occ_energy, vir_energy, coulomb, exch_kernel, minus_table
):
    vectors, nocc, own_virtual = trial_vectors.shape[1:]
    own_rows = occ_rows.shape[1]
    kpoints = lax.axis_size("ka")
    bands = lax.axis_size("band")
    self_point = lax.axis_index("ka").astype(jnp.int32).reshape(1)
    occ_own, vir_own = occ_rows[0], vir_rows[0]
    points = own_rows // kpoints
    width = vectors * nocc

    trial_rows = jnp.transpose(trial_vectors[0].astype(jnp.bfloat16), (2, 0, 1))
    trial_full = lax.all_gather(
        trial_rows.reshape(own_virtual, width), "band", axis=0, tiled=True
    )
    occ_all = lax.all_gather(occ_own, ("ka", "band"), axis=0, tiled=True)
    occ_all = occ_all.reshape(kpoints, bands * own_rows, nocc)

    mapped = jnp.dot(vir_own, trial_full, preferred_element_type=jnp.float32)
    y_own = mapped.astype(jnp.bfloat16)
    y_all = lax.all_to_all(
        y_own.reshape(kpoints, points, width), "ka", split_axis=0, concat_axis=0, tiled=True
    )
    occ_wide = occ_own.astype(jnp.float32)
    density_own = jnp.sum(
        y_own.astype(jnp.float32).reshape(own_rows, vectors, nocc) * occ_wide[:, None, :], axis=2
    )
    density_sum = lax.psum(density_own.T, "ka")
    density_half = lax.all_gather(density_sum.astype(jnp.bfloat16), "band", axis=1, tiled=True)
    potential = jnp.einsum("vn,rn->rv", density_half, coulomb, preferred_element_type=jnp.float32)

    z_all = exchange(self_point, minus_table, y_all, occ_all, exch_kernel)
    z_own = lax.all_to_all(z_all, "ka", split_axis=0, concat_axis=0, tiled=True)
    z_own = z_own.reshape(own_rows, vectors, nocc)
    coupling = 2.0 * potential[:, :, None] * occ_wide[:, None, :] - z_own.astype(jnp.float32)
    coupling = coupling.astype(jnp.bfloat16).reshape(own_rows, width)
    partial_sums = lax.dot_general(
        vir_own, coupling, (((0,), (0,)), ((), ())), preferred_element_type=jnp.float32
    )
    parts = lax.all_to_all(
        partial_sums.astype(jnp.bfloat16).reshape(bands, own_virtual, width),
        "band",
        split_axis=0,
        concat_axis=0,
        tiled=True,
    )
    coupled = jnp.sum(parts.astype(jnp.float32), axis=0).reshape(own_virtual, vectors, nocc)
    coupled = jnp.transpose(coupled, (1, 2, 0))
    energy_gaps = vir_energy[0][None, :] - occ_energy[0][:, None]
    return (energy_gaps[None] * trial_vectors[0] + coupled)[None]


def solution(mesh):
    in_specs = (
        P("ka", "band", None),
        P("ka", "band", None),
        P("ka", None, None, "band"),
        P("ka", None),
        P("ka", "band"),
        P("band", None),
        P(None, "band", None),
        P(),
    )
    out_specs = P("ka", None, None, "band")
    return jax.shard_map(
        per_device, mesh=mesh, in_specs=in_specs, out_specs=out_specs, check_vma=False
    )
```

time: 376 us -> 161 us (0.43)
  waiting for transfers between devices: 167 us -> 56 us
  blocking collectives: 102 us -> 53.6 us
  local copies, waits for them, and re-layouts: 35.4 us -> 4.62 us
  other arithmetic: 27.7 us -> 1.78 us
  matrix products: 20.5 us -> 4.67 us
  Pallas kernels: 0 us -> 14.1 us
    all_to_all x2 -> x3, waiting for transfers between devices: 95.2 us -> 16.6 us  [the longest x1 10.5 us: per_device(): lax.all_to_all(y_own.reshape(kpoints, points, width), 'ka', split_axis=0,...]
    psum x1, blocking collectives: 80 us -> 32.3 us  [per_device(): density_sum = lax.psum(density_own.T, 'ka')]
    reduce_scatter x1 -> x0, waiting for transfers between devices: 39.7 us -> none  [per_device(): lax.psum_scatter(partial_sums, 'band', scatter_dimension=2, tiled=True)]
    unnamed x2 -> x0, other arithmetic: 23.3 us -> none
    dot_general x4 -> x3, matrix products: 20.5 us -> 4.67 us  [the longest x1 2.35 us: per_device(): mapped = jnp.dot(vir_own, trial_full, preferred_element_type=jnp.float32)]
    gather x1 -> x0, local copies, waits for them, and re-layouts: 14.6 us -> none  [per_device(): jnp.take(lax.all_to_all(split_pairs, 'ka', split_axis=2, concat_axis=2, t...]
    pallas_call x0 -> x1, Pallas kernels: none -> 14.1 us  [exchange(): pl.pallas_call(exchange_kernel, grid_spec=grid_spec, out_shape=jax.ShapeD...]
    all_to_all x2 -> x0, local copies, waits for them, and re-layouts: 9 us -> none  [the longest x1 4.51 us: per_device(): lax.all_to_all(split_pairs, 'ka', split_axis=2, concat_axis=2, tiled=True)]
  transfers between devices with their start and end apart: 4 -> 4, of which waited for: 4 -> 3; matrix products, arithmetic and copies ran while one was open for 4% -> 4% of each run, Pallas kernels for 0% -> 0%
where the time goes in v1:
time: 161 us; the launch traced here: 160 us
  waiting for transfers between devices  56 us (35%)
  blocking collectives  53.6 us (33%)
  Pallas kernels  14.1 us (9%)
  between operations  13.6 us (8%)
  starting transfers between devices  11.8 us (7%)
  matrix products  4.67 us (3%)
  local copies, waits for them, and re-layouts  4.62 us (3%)
  other arithmetic  1.78 us (1%)
    all_gather x1, waiting for transfers between devices, per_device(): occ_all = lax.all_gather(occ_own, ('ka', 'band'), axis=0, tiled=True)  38.7 us
    psum x1, blocking collectives, per_device(): density_sum = lax.psum(density_own.T, 'ka')  32.3 us
    pallas_call x1, Pallas kernels, exchange(): pl.pallas_call(exchange_kernel, grid_spec=grid_spec, out_shape=jax.ShapeD...  14.1 us
    all_gather x1, blocking collectives, per_device(): lax.all_gather(trial_rows.reshape(own_virtual, width), 'band', axis=0, ti...  11.3 us
    all_to_all x1, waiting for transfers between devices, per_device(): lax.all_to_all(y_own.reshape(kpoints, points, width), 'ka', split_axis=0,...  10.5 us
    all_gather x1, blocking collectives, per_device(): lax.all_gather(density_sum.astype(jnp.bfloat16), 'band', axis=1, tiled=True)  10 us
    all_to_all x1, waiting for transfers between devices, per_device(): lax.all_to_all(partial_sums.astype(jnp.bfloat16).reshape(bands, own_virtu...  6.07 us
    all_to_all x1, starting transfers between devices, per_device(): lax.all_to_all(y_own.reshape(kpoints, points, width), 'ka', split_axis=0,...  4.88 us
  transfers between devices with their start and end apart: 4, of which 3 were waited for; matrix products, arithmetic and copies ran while one was open for 4% of the time, Pallas kernels for 0%

profile of v1, /device:TPU:0, one launch (start us, length us, event | category | flops | bytes accessed | tf_op | source)
XLA Modules:
  0.0 160.1 jit_solution(12075279484808820407)
XLA Ops:
  6.5 0.7 all-gather.3.cloned.1.call-update
  7.3 1.1 copy.23
  8.4 11.3 %all_gather.9 = bf16[896,256]{1,0:T(8,128)(2,1)S(1)} all-gather(bf16[224,256]{1,0:T(8,128)(2,1)S(1)} %bitcast.45), channel_id=1, replica_groups=mesh['ka'=8,'band'=4] {'band'}, dimensions={0}, use_global_device_ids=true | all-gather | bytes 573440 | tf_op jit(solution)/shard_map/all_gather | solution.py:113
  19.7 2.3 %convolution_convert_fusion.1 = bf16[512,256]{1,0:T(8,128)(2,1)} fusion(bf16[896,256]{1,0:T(8,128)(2,1)S(1)} %all_gather.9, bf16[1,512,896]{2,1,0:T(8,128)(2,1)} %param.9), kind=kOutput, calls=%fused_computation.2 | convolution fusion | flops 235012096 | bytes 1638400 | tf_op jit(solution)/shard_map/dot_general | solution.py:119
  22.0 4.9 %all-to-all-start = ((bf16[8,64,256]{2,1,0:T(8,128)(2,1)}), bf16[8,64,256]{2,1,0:T(8,128)(2,1)S(1)}, u32[]{:S(2)}, u32[]{:S(2)}) async-start(bf16[8,64,256]{2,1,0:T(8,128)(2,1)} %bitcast.9), calls=%async_computation | async-start | bytes 524288 | tf_op jit(solution)/shard_map/all_to_all | solution.py:121
  26.9 10.5 %all-to-all-done.y_ref = bf16[8,64,256]{2,1,0:T(8,128)(2,1)S(1)} async-done(((bf16[8,64,256]{2,1,0:T(8,128)(2,1)}), bf16[8,64,256]{2,1,0:T(8,128)(2,1)S(1)}, u32[]{:S(2)}, u32[]{:S(2)}) %all-to-all-start) | async-done | bytes 262176 | tf_op jit(solution)/shard_map/all_to_all | solution.py:121
  37.4 38.7 %all-gather.3.cloned.1.call-done = bf16[1,16384,128]{2,1,0:T(8,128)(2,1)} async-done(((bf16[1,512,128]{2,1,0:T(8,128)(2,1)}), bf16[1,16384,128]{2,1,0:T(8,128)(2,1)}) %all-gather.3.cloned.1.call-update) | async-done | bytes 4194320 | tf_op jit(solution)/shard_map/all_gather | solution.py:116
  76.1 14.1 %shard_map.85 = bf16[8,64,256]{2,1,0:T(8,128)(2,1)} custom-call(s32[1]{0:T(128)} %bitcast.8.self_ref, s32[8,8]{1,0:T(8,128)} %table_ref.1, bf16[8,64,256]{2,1,0:T(8,128)(2,1)} %copy-done.3, bf16[8,2048,128]{2,1,0:T(8,128)(2,1)} %bitcast.49, bf16[8,512,2048]{2,1,0:T(8,128)(2,1)} %exch_ref.1), custom_call_target="tpu_custom_call" | custom-call | flops 17179869184 | bytes 6291456 | tf_op jit(solution)/shard_map/pallas_call | solution.py:87
  90.2 3.4 %all-to-all-start.1 = ((bf16[8,64,256]{2,1,0:T(8,128)(2,1)}), bf16[8,64,256]{2,1,0:T(8,128)(2,1)S(1)}, u32[]{:S(2)}, u32[]{:S(2)}) async-start(bf16[8,64,256]{2,1,0:T(8,128)(2,1)} %shard_map.85), calls=%async_computation.1 | async-start | bytes 524288 | tf_op jit(solution)/shard_map/all_to_all | solution.py:133
  93.7 1.2 reshape.94
  94.9 0.6 multiply_reduce_fusion
  95.5 32.3 %psum.7 = bf16[2,512]{0,1:T(8,128)(2,1)S(1)} all-reduce(f32[2,512]{0,1:T(8,128)S(1)} %bitcast.44), channel_id=1, replica_groups=mesh['ka'=8,'band'=4] {'ka'}, use_global_device_ids=true, to_apply=%region_1.0 | all-reduce | flops 1024 | bytes 6144 | tf_op jit(solution)/shard_map/psum | solution.py:128
  127.8 10.0 %all_gather.10 = bf16[2,2048]{0,1:T(8,128)(2,1)S(1)} all-gather(bf16[2,512]{0,1:T(8,128)(2,1)S(1)} %psum.7), channel_id=1, replica_groups=mesh['ka'=8,'band'=4] {'band'}, dimensions={1}, use_global_device_ids=true | all-gather | bytes 10240 | tf_op jit(solution)/shard_map/all_gather | solution.py:129
  137.8 0.6 fusion.1
  138.5 0.2 copy.11
  138.7 0.3 reshape.95
  139.0 0.7 subtract_convert_fusion
  139.7 1.7 %fusion = bf16[896,256]{0,1:T(8,128)(2,1)S(1)} fusion(bf16[1,512,896]{2,1,0:T(8,128)(2,1)} %param.9, bf16[64,8,2,128]{3,2,1,0:T(2,128)(2,1)S(1)} %bitcast.43), kind=kOutput, calls=%fused_computation.1 | convolution fusion | flops 235110400 | bytes 1638400 | tf_op jit(solution)/shard_map/dot_general | solution.py:137
  141.4 1.0 copy.12
  142.4 3.5 %all-to-all-start.2 = ((bf16[4,224,256]{2,1,0:T(8,128)(2,1)}), bf16[4,224,256]{2,1,0:T(8,128)(2,1)S(1)}, u32[]{:S(2)}, u32[]{:S(2)}) async-start(bf16[4,224,256]{2,1,0:T(8,128)(2,1)} %bitcast.12), calls=%async_computation.2 | async-start | bytes 917504 | tf_op jit(solution)/shard_map/all_to_all | solution.py:140
  146.0 6.1 %all-to-all-done.2 = bf16[4,224,256]{2,1,0:T(8,128)(2,1)S(1)} async-done(((bf16[4,224,256]{2,1,0:T(8,128)(2,1)}), bf16[4,224,256]{2,1,0:T(8,128)(2,1)S(1)}, u32[]{:S(2)}, u32[]{:S(2)}) %all-to-all-start.2) | async-done | bytes 458784 | tf_op jit(solution)/shard_map/all_to_all | solution.py:140
  152.1 0.1 reshape.92
  152.2 0.3 fusion.6
  152.5 0.7 copy.13
  (18 shorter events, 0.2 us)
Async XLA Ops:
  6.5 131.3 %copy-start = (bf16[512,2048]{1,0:T(8,128)(2,1)S(1)}, bf16[512,2048]{1,0:T(8,128)(2,1)}, u32[]{:S(2)}) copy-start(bf16[512,2048]{1,0:T(8,128)(2,1)} %param.13) | copy-start | bytes 6291460
  6.5 69.6 %all-gather.3.cloned.1.call-start = ((), (), s32[]{:S(2)}) async-start(), calls=%async_computation.3 | async-start | bytes 4325376 | tf_op jit(solution)/shard_map/all_gather | solution.py:116
  22.0 15.4 %all-to-all-start = ((bf16[8,64,256]{2,1,0:T(8,128)(2,1)}), bf16[8,64,256]{2,1,0:T(8,128)(2,1)S(1)}, u32[]{:S(2)}, u32[]{:S(2)}) async-start(bf16[8,64,256]{2,1,0:T(8,128)(2,1)} %bitcast.9), calls=%async_computation | async-start | bytes 524288 | tf_op jit(solution)/shard_map/all_to_all | solution.py:121
  37.4 38.7 %copy-start.3 = (bf16[8,64,256]{2,1,0:T(8,128)(2,1)}, bf16[8,64,256]{2,1,0:T(8,128)(2,1)S(1)}, u32[]{:S(2)}) copy-start(bf16[8,64,256]{2,1,0:T(8,128)(2,1)S(1)} %all-to-all-done.y_ref) | copy-start | bytes 786436
  76.1 17.5 %copy-start.2 = (bf16[1,512,128]{2,1,0:T(8,128)(2,1)S(1)}, bf16[1,512,128]{2,1,0:T(8,128)(2,1)}, u32[]{:S(2)}) copy-start(bf16[1,512,128]{2,1,0:T(8,128)(2,1)} %param.8) | copy-start | bytes 393220
  90.2 48.5 %all-to-all-start.1 = ((bf16[8,64,256]{2,1,0:T(8,128)(2,1)}), bf16[8,64,256]{2,1,0:T(8,128)(2,1)S(1)}, u32[]{:S(2)}, u32[]{:S(2)}) async-start(bf16[8,64,256]{2,1,0:T(8,128)(2,1)} %shard_map.85), calls=%async_computation.1 | async-start | bytes 524288 | tf_op jit(solution)/shard_map/all_to_all | solution.py:133
  138.9 6.9 %copy-start.4 = (f32[1,224]{1,0:T(1,128)S(1)}, f32[1,224]{1,0:T(1,128)}, u32[]{:S(2)}) copy-start(f32[1,224]{1,0:T(1,128)} %param.12) | copy-start | bytes 2692
  139.0 6.9 %copy-start.5 = (f32[1,128]{1,0:T(1,128)S(1)}, f32[1,128]{1,0:T(1,128)}, u32[]{:S(2)}) copy-start(f32[1,128]{1,0:T(1,128)} %param.11) | copy-start | bytes 1540
  139.7 12.5 %copy-start.1 = (f32[1,2,128,224]{2,3,1,0:T(8,128)S(1)}, f32[1,2,128,224]{2,3,1,0:T(8,128)}, u32[]{:S(2)}) copy-start(f32[1,2,128,224]{2,3,1,0:T(8,128)} %param.10) | copy-start | bytes 688132
  142.4 9.7 %all-to-all-start.2 = ((bf16[4,224,256]{2,1,0:T(8,128)(2,1)}), bf16[4,224,256]{2,1,0:T(8,128)(2,1)S(1)}, u32[]{:S(2)}, u32[]{:S(2)}) async-start(bf16[4,224,256]{2,1,0:T(8,128)(2,1)} %bitcast.12), calls=%async_computation.2 | async-start | bytes 917504 | tf_op jit(solution)/shard_map/all_to_all | solution.py:140
Sparse Core Ops, SparseCore 0:
  10.2 65.8 all-gather.2
